TPU v7x, 32 devices: a whole 2x2x4 slice. The times are simulated.
32 devices in a mesh: gx: 8 (over z, y), gy: 4 (over x, core).
Axes of the slice: x: 2, y: 2, z: 4, core: 2. Of those that a mesh axis runs over, the one named last changes fastest.
Arguments:
- charge_density: float32 [256, 256, 256], P('gx', 'gy'), may hold values from -5080 to 5140
Outputs:
- potential: float32 [256, 256, 256], P('gx', 'gy')
- energies: float32 [2], replicated
All inputs are finite; a program needn't handle non-finite values.
Results may differ from a plain program's by a relative error of at most 0.0003.
Values sent between devices are 32-bit elements.
A program may use at most 192 MiB of HBM per device.

v0:
```python
import math
import jax
import jax.numpy as jnp
import numpy as np
from jax import lax
from jax.sharding import PartitionSpec as P

ORDER = 16
exact_mode = lax.Precision.HIGHEST
outer_ratio = 1.1
radius_scale = math.sqrt(3.0) / 2.0


def sine_table(length):
    counter = jnp.arange(length, dtype=jnp.int32) + 1
    product = counter[:, None] * counter[None, :] % (2 * (length + 1))
    return jnp.sin(math.pi * product.astype(jnp.float32) / (length + 1))


def eigen_line(counter, length):
    half_angle = math.pi * (counter + 1).astype(jnp.float32) / (2.0 * (length + 1))
    return 4.0 * float((length + 1) * (length + 1)) * jnp.sin(half_angle) ** 2


def recurrence_tables():
    degree_count = ORDER + 1
    near_coeff = np.zeros((degree_count, degree_count, 1), np.float32)
    far_coeff = np.zeros((degree_count, degree_count, 1), np.float32)
    sector = np.ones(degree_count, np.float32)
    for degree in range(1, degree_count):
        for azimuth in range(degree):
            divisor = math.sqrt(degree * degree - azimuth * azimuth)
            near_coeff[degree, azimuth, 0] = (2 * degree - 1) / divisor
            far_coeff[degree, azimuth, 0] = (
                math.sqrt((degree - 1) * (degree - 1) - azimuth * azimuth) / divisor
            )
        if degree >= 2:
            sector[degree] = math.sqrt((2 * degree - 1) / (2.0 * degree))
    return (near_coeff, far_coeff, sector)


def expansion_weights():
    degree_count = ORDER + 1
    weights = np.zeros((degree_count, degree_count), np.float32)
    for degree in range(degree_count):
        for azimuth in range(degree + 1):
            factor = 1.0 if azimuth == 0 else 2.0
            weights[degree, azimuth] = factor / (
                4.0 * math.pi * radius_scale * outer_ratio ** (degree + 1)
            )
    return weights


def harmonic_sweep(unit_x, unit_y, unit_z, visitor, running):
    near_coeff, far_coeff, sector = recurrence_tables()
    degree_count = ORDER + 1
    selector = np.eye(degree_count, dtype=np.float32)[:, :, None]
    empty_rows = jnp.zeros((degree_count,) + unit_x.shape, unit_x.dtype)
    sector_cosine = jnp.ones_like(unit_x)
    sector_sine = jnp.zeros_like(unit_x)
    cosine_prev, sine_prev, cosine_old, sine_old = (empty_rows, empty_rows, empty_rows, empty_rows)
    for degree in range(degree_count):
        if degree > 0:
            sector_cosine, sector_sine = (
                sector[degree] * (unit_x * sector_cosine - unit_y * sector_sine),
                sector[degree] * (unit_x * sector_sine + unit_y * sector_cosine),
            )
        cosine_now = (
            near_coeff[degree] * unit_z * cosine_prev
            - far_coeff[degree] * cosine_old
            + selector[degree] * sector_cosine
        )
        sine_now = (
            near_coeff[degree] * unit_z * sine_prev
            - far_coeff[degree] * sine_old
            + selector[degree] * sector_sine
        )
        running = visitor(running, degree, cosine_now, sine_now)
        cosine_old, sine_old = (cosine_prev, sine_prev)
        cosine_prev, sine_prev = (cosine_now, sine_now)
    return running


def face_moments(point_x, point_y, point_z, charge):
    radius = jnp.sqrt(point_x * point_x + point_y * point_y + point_z * point_z)
    scaled_radius = radius / radius_scale

    def visitor(running, degree, cosine_now, sine_now):
        weight, moment_cosine, moment_sine, facing_cosine, facing_sine = running
        moment_cosine = moment_cosine + [jnp.dot(cosine_now, weight, precision=exact_mode)]
        moment_sine = moment_sine + [jnp.dot(sine_now, weight, precision=exact_mode)]
        facing_cosine = facing_cosine + [jnp.dot(cosine_now, charge, precision=exact_mode)]
        facing_sine = facing_sine + [jnp.dot(sine_now, charge, precision=exact_mode)]
        return (weight * scaled_radius, moment_cosine, moment_sine, facing_cosine, facing_sine)

    result = harmonic_sweep(
        point_x / radius, point_y / radius, point_z / radius, visitor, (charge, [], [], [], [])
    )
    return tuple((jnp.stack(listing) for listing in result[1:]))


def face_potential(point_x, point_y, point_z, weight_cosine, weight_sine):
    radius = jnp.sqrt(point_x * point_x + point_y * point_y + point_z * point_z)

    def visitor(accum, degree, cosine_now, sine_now):
        accum = accum + jnp.dot(weight_cosine[degree], cosine_now, precision=exact_mode)
        return accum + jnp.dot(weight_sine[degree], sine_now, precision=exact_mode)

    return harmonic_sweep(
        point_x / radius, point_y / radius, point_z / radius, visitor, jnp.zeros_like(point_x)
    )


def moments_of(points):
    return face_moments(points[0], points[1], points[2], points[3])


def no_moments(points):
    empty_rows = jnp.zeros((ORDER + 1, ORDER + 1), jnp.float32)
    return (empty_rows, empty_rows, empty_rows, empty_rows)


def potential_of(points):
    return face_potential(points[0], points[1], points[2], points[3], points[4])


def no_potential(points):
    return jnp.zeros_like(points[0])


def forward(volume, sine_rows, swap_one, swap_two):
    cells_a, cells_b, length = volume.shape
    spectrum = jnp.einsum("abz,zk->kab", volume, sine_rows, precision=exact_mode)
    spectrum = swap_one(spectrum.reshape(length, cells_a * cells_b))
    groups_one = spectrum.shape[1] // (cells_a * cells_b)
    pieces = spectrum.reshape(spectrum.shape[0], groups_one, cells_a, cells_b)
    table_one = sine_rows.reshape(groups_one, cells_b, length)
    spectrum = jnp.einsum("zpab,pbj->jza", pieces, table_one, precision=exact_mode)
    depth_cells = spectrum.shape[1]
    spectrum = swap_two(spectrum.reshape(length, depth_cells * cells_a))
    groups_two = spectrum.shape[1] // (depth_cells * cells_a)
    pieces = spectrum.reshape(spectrum.shape[0], groups_two, depth_cells, cells_a)
    table_two = sine_rows.reshape(groups_two, cells_a, length)
    return jnp.einsum("kqzc,qcj->kzj", pieces, table_two, precision=exact_mode)


def inverse(spectrum, sine_rows, back_two, back_one, cells_a, cells_b):
    rows_one, depth_cells, length = spectrum.shape
    groups_two = length // cells_a
    groups_one = length // cells_b
    table_two = sine_rows.reshape(length, groups_two, cells_a)
    pieces = jnp.einsum("kzj,jqc->kqzc", spectrum, table_two, precision=exact_mode)
    pieces = back_two(pieces.reshape(rows_one, groups_two * depth_cells * cells_a))
    pieces = pieces.reshape(length, depth_cells, cells_a)
    table_one = sine_rows.reshape(length, groups_one, cells_b)
    volume = jnp.einsum("jza,jpb->zpab", pieces, table_one, precision=exact_mode)
    volume = back_one(volume.reshape(depth_cells, groups_one * cells_a * cells_b))
    volume = volume.reshape(length, cells_a, cells_b)
    return jnp.einsum("kab,kz->abz", volume, sine_rows, precision=exact_mode)


def shards(charge_density):
    cells_a, cells_b, length = charge_density.shape
    spacing = 1.0 / (length + 1)
    sine_rows = sine_table(length)
    index_x = lax.axis_index("gx")
    index_y = lax.axis_index("gy")

    def swap_one(operand):
        return lax.all_to_all(operand, "gy", split_axis=0, concat_axis=1, tiled=True)

    def swap_two(operand):
        return lax.all_to_all(operand, "gx", split_axis=0, concat_axis=1, tiled=True)

    def back_two(operand):
        return lax.all_to_all(operand, "gx", split_axis=1, concat_axis=0, tiled=True)

    def back_one(operand):
        return lax.all_to_all(operand, "gy", split_axis=1, concat_axis=0, tiled=True)

    groups_one = lax.axis_size("gy")
    groups_two = lax.axis_size("gx")
    count_one = length // groups_two
    count_two = length // groups_one
    eigen_one = eigen_line(index_x * count_one + jnp.arange(count_one, dtype=jnp.int32), length)
    eigen_two = eigen_line(index_y * count_two + jnp.arange(count_two, dtype=jnp.int32), length)
    eigen_full = eigen_line(jnp.arange(length, dtype=jnp.int32), length)
    denominator = (
        eigen_one[:, None, None] + eigen_two[None, :, None] + eigen_full[None, None, :]
    ) * ((length + 1) / 2.0) ** 3

    def back_of(spectrum):
        return inverse(spectrum, sine_rows, back_two, back_one, cells_a, cells_b)

    charge_spectrum = forward(charge_density, sine_rows, swap_one, swap_two) / denominator
    first_field = back_of(charge_spectrum)
    energy_first = spacing**3 * jnp.sum(charge_density * first_field)
    coords_x = (
        (index_x * cells_a + jnp.arange(cells_a, dtype=jnp.int32)).astype(jnp.float32)
        - (length - 1) / 2.0
    ) * spacing
    coords_y = (
        (index_y * cells_b + jnp.arange(cells_b, dtype=jnp.int32)).astype(jnp.float32)
        - (length - 1) / 2.0
    ) * spacing
    coords_z = (jnp.arange(length, dtype=jnp.float32) - (length - 1) / 2.0) * spacing
    face_x = jnp.broadcast_to(coords_x[:, None], (cells_a, cells_b)).reshape(-1)
    face_y = jnp.broadcast_to(coords_y[None, :], (cells_a, cells_b)).reshape(-1)
    plane_z = jnp.full((cells_a * cells_b,), 0.5, jnp.float32)
    side_y = jnp.broadcast_to(coords_y[:, None], (cells_b, length)).reshape(-1)
    side_depth_b = jnp.broadcast_to(coords_z[None, :], (cells_b, length)).reshape(-1)
    plane_b = jnp.full((cells_b * length,), 0.5, jnp.float32)
    side_x = jnp.broadcast_to(coords_x[:, None], (cells_a, length)).reshape(-1)
    side_depth_a = jnp.broadcast_to(coords_z[None, :], (cells_a, length)).reshape(-1)
    plane_a = jnp.full((cells_a * length,), 0.5, jnp.float32)
    boundary_faces = [
        (face_x, face_y, -plane_z, first_field[:, :, 0], None),
        (face_x, face_y, plane_z, first_field[:, :, -1], None),
        (-plane_b, side_y, side_depth_b, first_field[0], index_x == 0),
        (plane_b, side_y, side_depth_b, first_field[-1], index_x == lax.axis_size("gx") - 1),
        (side_x, -plane_a, side_depth_a, first_field[:, 0], index_y == 0),
        (side_x, plane_a, side_depth_a, first_field[:, -1], index_y == lax.axis_size("gy") - 1),
    ]
    totals = None
    for point_x, point_y, point_z, near_cells, owning in boundary_faces:
        points = (point_x, point_y, point_z, spacing * near_cells.reshape(-1))
        if owning is None:
            face_terms = moments_of(points)
        else:
            face_terms = lax.cond(owning, moments_of, no_moments, points)
        if totals is None:
            totals = face_terms
        else:
            totals = tuple((earlier + later for earlier, later in zip(totals, face_terms)))
    mom_cosine, mom_sine, dir_cosine, dir_sine = totals
    sum_cosine, sum_sine = lax.psum((mom_cosine, mom_sine), ("gx", "gy"))
    weights = expansion_weights()
    weight_cosine = weights * sum_cosine
    weight_sine = weights * sum_sine
    potentials = []
    for point_x, point_y, point_z, near_cells, owning in boundary_faces:
        points = (point_x, point_y, point_z, weight_cosine, weight_sine)
        if owning is None:
            potentials.append(potential_of(points) / spacing**2)
        else:
            potentials.append(lax.cond(owning, potential_of, no_potential, points) / spacing**2)
    planes = jnp.stack(
        [potentials[0].reshape(cells_a, cells_b), potentials[1].reshape(cells_a, cells_b)]
    )
    lead_walls = jnp.stack(
        [potentials[4].reshape(cells_a, length), potentials[5].reshape(cells_a, length)]
    )
    tail_walls = jnp.stack(
        [potentials[2].reshape(cells_b, length), potentials[3].reshape(cells_b, length)]
    )
    plane_width = 2 * cells_a * cells_b // count_two
    plane_part = jnp.broadcast_to(
        planes.reshape(1, count_two, plane_width), (groups_one, count_two, plane_width)
    ).reshape(length, plane_width)
    lead_depth = jnp.einsum("ftz,zk->kft", lead_walls, sine_rows, precision=exact_mode).reshape(
        length, 2 * cells_a
    )
    tail_depth = jnp.einsum("fbz,zk->kfb", tail_walls, sine_rows, precision=exact_mode).reshape(
        length, 2 * cells_b
    )
    received = swap_one(jnp.concatenate([plane_part, lead_depth, tail_depth], axis=1))
    received = received.reshape(count_two, groups_one, -1)
    plane_all = jnp.transpose(received[:, :, :plane_width], (1, 0, 2)).reshape(
        groups_one, 2, cells_a, cells_b
    )
    lead_total = jnp.sum(
        received[:, :, plane_width : plane_width + 2 * cells_a].reshape(
            count_two, groups_one, 2, cells_a
        ),
        axis=1,
    )
    tail_part = received[:, :, plane_width + 2 * cells_a :].reshape(
        count_two, groups_one, 2, cells_b
    )
    lead_table = sine_rows.reshape(groups_one, cells_b, length)
    plane_lead = jnp.einsum("pftb,pbj->jft", plane_all, lead_table, precision=exact_mode).reshape(
        length, 2 * cells_a
    )
    tail_lead = jnp.einsum("kpfb,pbj->jfk", tail_part, lead_table, precision=exact_mode).reshape(
        length, 2 * count_two
    )
    lead_width = 2 * count_two * cells_a // count_one
    lead_copies = jnp.broadcast_to(
        lead_total.reshape(1, count_one, lead_width), (groups_two, count_one, lead_width)
    ).reshape(length, lead_width)
    received = swap_two(jnp.concatenate([plane_lead, lead_copies, tail_lead], axis=1))
    received = received.reshape(count_one, groups_two, -1)
    tail_table = sine_rows.reshape(groups_two, cells_a, length)
    plane_modes = jnp.einsum(
        "jqft,qtm->jfm",
        received[:, :, : 2 * cells_a].reshape(count_one, groups_two, 2, cells_a),
        tail_table,
        precision=exact_mode,
    )
    lead_all = jnp.transpose(
        received[:, :, 2 * cells_a : 2 * cells_a + lead_width], (1, 0, 2)
    ).reshape(groups_two, count_two, 2, cells_a)
    lead_modes = jnp.einsum("qkft,qtm->fkm", lead_all, tail_table, precision=exact_mode)
    tail_modes = jnp.sum(
        received[:, :, 2 * cells_a + lead_width :].reshape(count_one, groups_two, 2, count_two),
        axis=1,
    )
    edge_rows = jnp.stack([sine_rows[0], sine_rows[-1]])
    depth_edge = lax.dynamic_slice_in_dim(edge_rows, index_y * count_two, count_two, 1)
    mode_edge = lax.dynamic_slice_in_dim(edge_rows, index_x * count_one, count_one, 1)
    result = jnp.einsum("jfm,fk->jkm", plane_modes, depth_edge, precision=exact_mode)
    result = result + jnp.einsum("fj,fkm->jkm", mode_edge, lead_modes, precision=exact_mode)
    potential = back_of(
        charge_spectrum
        + (result + jnp.einsum("jfk,fm->jkm", tail_modes, edge_rows, precision=exact_mode))
        / denominator
    )
    first_energy, second_energy = lax.psum(
        (energy_first, spacing**3 * jnp.sum(charge_density * potential)), ("gx", "gy")
    )
    return (potential, jnp.stack([first_energy, second_energy]))


def solution(mesh):
    placed = (P("gx", "gy", None),)
    return jax.shard_map(
        shards, mesh=mesh, in_specs=placed, out_specs=(P("gx", "gy", None), P()), check_vma=False
    )
```

profile of v0, /device:TPU:0, one launch (start us, length us, event | category | flops | bytes accessed | tf_op | source)
XLA Modules:
  0.0 1063.5 jit_solution(1481408688920894633)
XLA Ops:
  0.6 4.5 fusion.1266
  8.2 4.7 copy.900
  13.0 4.2 all-to-all-start
  17.3 25.6 %all-to-all-done = f32[4,64,2048]{2,1,0:T(8,128)S(1)} async-done(((f32[4,64,2048]{2,1,0:T(8,128)}), f32[4,64,2048]{2,1,0:T(8,128)S(1)}, u32[]{:S(2)}, u32[]{:S(2)}) %all-to-all-start) | async-done | bytes 2097184 | tf_op jit(solution)/shard_map/all_to_all | solution.py:170
  45.9 9.2 convolution_bitcast_fusion
  55.1 6.9 all-to-all-start.1
  62.3 59.0 %all-to-all-done.1 = f32[8,32,2048]{2,1,0:T(8,128)S(1)} async-done(((f32[8,32,2048]{2,1,0:T(8,128)}), f32[8,32,2048]{2,1,0:T(8,128)S(1)}, u32[]{:S(2)}, u32[]{:S(2)}) %all-to-all-start.1) | async-done | bytes 2097184 | tf_op jit(solution)/shard_map/all_to_all | solution.py:173
  121.3 4.8 reshape.2046
  126.1 11.5 %bitcast_divide_fusion = f32[32,64,256]{2,1,0:T(8,128)S(1)} fusion(f32[32,8,64,32]{3,2,0,1:T(8,128)} %reshape.2046, f32[256]{0:T(256)S(1)} %multiply_multiply_fusion.64, f32[32,64]{1,0:T(8,128)S(1)} %broadcast_add_fusion, s32[256]{0:T(256)S(1)} %iota_add_fusion, s32[8,32]{1,0:T(8,128)S(1)} %add_add_fusion.7), kind=kOutput, calls=%fused_computation.1785 | convolution fusion | flops 1612775424 | bytes 4205568 | tf_op jit(solution)/shard_map/kqzc,qcj->kzj/dot_general | solution.py:144
  139.0 7.1 convolution_bitcast_fusion.2
  146.1 6.9 copy.905
  153.0 7.5 reshape.2047
  160.5 3.6 all-to-all-start.2
  164.3 48.2 %all-to-all-done.2 = f32[32,8,2048]{2,0,1:T(8,128)S(1)} async-done(((f32[32,8,2048]{2,0,1:T(8,128)}), f32[32,8,2048]{2,0,1:T(8,128)S(1)}, u32[]{:S(2)}, u32[]{:S(2)}) %all-to-all-start.2) | async-done | bytes 2097184 | tf_op jit(solution)/shard_map/all_to_all | solution.py:176
  212.5 4.8 reshape.1197
  217.3 7.0 copy.872
  224.3 7.0 fusion.1211
  231.3 3.8 copy.873
  235.1 3.6 all-to-all-start.3
  241.1 23.2 %all-to-all-done.3 = f32[64,4,2048]{2,0,1:T(8,128)S(1)} async-done(((f32[64,4,2048]{2,0,1:T(8,128)}), f32[64,4,2048]{2,0,1:T(8,128)S(1)}, u32[]{:S(2)}, u32[]{:S(2)}) %all-to-all-start.3) | async-done | bytes 2097184 | tf_op jit(solution)/shard_map/all_to_all | solution.py:179
  264.3 11.5 %reshape.1198 = f32[256,32,64]{2,1,0:T(8,128)} reshape(f32[4,64,2048]{2,1,0:T(8,128)S(1)} %bitcast.2772) | data formatting | bytes 4194304 | tf_op jit(solution)/shard_map/reshape | solution.py:158
  275.8 11.3 %fusion.1202 = f32[32,64,256]{2,1,0:T(8,128)S(1)} fusion(f32[256,32,64]{2,1,0:T(8,128)} %reshape.1198, s32[256]{0:T(256)S(1)} %iota_add_fusion), kind=kOutput, calls=%fused_computation.1780 | convolution fusion | flops 1611202560 | bytes 4195328 | tf_op jit(solution)/shard_map/kab,kz->abz/dot_general | solution.py:159
  373.3 10.0 conditional.9
  383.3 113.1 %conditional.8 = (f32[17,17]{1,0:T(8,128)S(1)}, f32[17,17]{1,0:T(8,128)S(1)}) conditional(s32[]{:T(128)} %convert_element_type.118, () %tuple.64, (f32[17,1]{0,1:T(1,128)S(1)}, f32[16384]{0:T(1024)}, f32[16384]{0:T(1024)S(1)}, f32[16384]{0:T(1024)S(1)}, f32[17,1]{0,1:T(1,128)S(1)}, /*index=5*/f32[17,1]{0,1:T(1,128)S(1)}, ...), branch_computations={%region_0.1_spmd, %region_1.2_spmd} | conditional | flops 290816064 | bytes 57925084 | solution.py:230
  391.5 4.6 fusion.115
  396.1 4.5 fusion.114
  400.6 4.3 fusion.113
  404.9 4.1 fusion.112
  409.0 3.7 fusion.109
  412.7 4.0 fusion.108
  416.7 3.5 fusion.107
  420.1 3.5 fusion.106
  429.9 3.2 fusion.77
  440.8 6.4 multiply_add_fusion.2
  468.2 3.9 stack.481
  472.0 7.8 multiply_add_fusion.17
  497.0 16.6 %conditional.11 = (f32[17,17]{1,0:T(8,128)S(1)}, f32[17,17]{1,0:T(8,128)S(1)}) conditional(s32[]{:T(128)} %convert_element_type.121, () %tuple.69, (f32[17,1]{0,1:T(1,128)S(1)}, f32[8192]{0:T(1024)S(1)}, f32[8192]{0:T(1024)S(1)}, f32[8192]{0:T(1024)S(1)}, f32[17,1]{0,1:T(1,128)S(1)}, /*index=5*/f32[17,1]{0,1:T(1,128)S(1)}, ...), branch_computations={%region_6.7_spmd, %region_7.8_spmd} | conditional | flops 145408080 | bytes 28004404 | solution.py:230
  514.2 54.3 %conditional.10 = (f32[17,17]{1,0:T(8,128)}, f32[17,17]{1,0:T(8,128)}) conditional(s32[]{:T(128)} %convert_element_type.120, () %tuple.67, (f32[17,1]{0,1:T(1,128)S(1)}, f32[8192]{0:T(1024)S(1)}, f32[8192]{0:T(1024)S(1)}, f32[8192]{0:T(1024)S(1)}, f32[17,1]{0,1:T(1,128)S(1)}, /*index=5*/f32[17,1]{0,1:T(1,128)S(1)}, f32[32,64,256]{2,1,0:T(8,128)S(1)}, ...), branch_computations={%region_4.5_spmd, %region_5.6_spmd} | conditional | flops 145408080 | bytes 27208952 | solution.py:230
  577.8 40.4 %all-reduce.1 = (f32[17,17]{1,0:T(8,128)S(1)}, f32[17,17]{1,0:T(8,128)S(1)}) all-reduce(f32[17,17]{1,0:T(8,128)S(1)} %get-tuple-element.3281, f32[17,17]{1,0:T(8,128)S(1)} %get-tuple-element.3280), channel_id=1, replica_groups=mesh['gx'=8,'gy'=4] {'gx','gy'}, use_global_device_ids=true, to_apply=%region_8.9 | all-reduce | flops 578 | bytes 4624 | tf_op jit(solution)/shard_map/psum | solution.py:236
  658.0 10.0 conditional.13
  668.6 48.3 %conditional.12 = (f32[8192]{0:T(1024)S(1)}) conditional(s32[]{:T(128)} %convert_element_type.120, () %tuple.70, (f32[17,1]{0,1:T(1,128)S(1)}, f32[8192]{0:T(1024)S(1)}, f32[8192]{0:T(1024)S(1)}, f32[8192]{0:T(1024)S(1)}, f32[17,1]{0,1:T(1,128)S(1)}, /*index=5*/f32[17,1]{0,1:T(1,128)S(1)}, f32[17,17]{1,0:T(8,128)S(1)}, f32[17,1]{0,1:T(1,128)S(1)}, ...), branch_computations={%region_10.11_spmd, %region_11.12_spmd} | conditional | flops 145293392 | bytes 33228644 | solution.py:246
  718.3 15.7 %conditional.15 = (f32[16384]{0:T(1024)S(1)}) conditional(s32[]{:T(128)} %convert_element_type.119, () %tuple.75, (f32[17,1]{0,1:T(1,128)S(1)}, f32[16384]{0:T(1024)}, f32[16384]{0:T(1024)S(1)}, f32[16384]{0:T(1024)S(1)}, f32[17,1]{0,1:T(1,128)S(1)}, /*index=5*/f32[17,1]{0,1:T(1,128)S(1)}, f32[17,17]{1,0:T(8,128)S(1)}, f32[17,1]{0,1:T(1,128)S(1)}, ...), branch_computations={%region_16.17_spmd, %region_17.18_spmd} | conditional | flops 290586688 | bytes 66294256 | solution.py:246
  734.0 81.9 %conditional.14 = (f32[16384]{0:T(1024)S(1)}) conditional(s32[]{:T(128)} %convert_element_type.118, () %tuple.73, (f32[17,1]{0,1:T(1,128)S(1)}, f32[16384]{0:T(1024)}, f32[16384]{0:T(1024)S(1)}, f32[16384]{0:T(1024)S(1)}, f32[17,1]{0,1:T(1,128)S(1)}, /*index=5*/f32[17,1]{0,1:T(1,128)S(1)}, f32[17,17]{1,0:T(8,128)S(1)}, f32[17,1]{0,1:T(1,128)S(1)}, ...), branch_computations={%region_14.15_spmd, %region_15.16_spmd} | conditional | flops 290586688 | bytes 66291856 | solution.py:246
  738.7 3.9 fusion.948
  742.6 3.8 fusion.950
  746.4 3.6 fusion.952
  750.0 3.4 fusion.954
  759.3 3.5 fusion.958
  778.1 6.4 multiply_add_fusion.334
  796.8 6.5 multiply_add_fusion.335
  820.3 23.6 %all_to_all.119 = f32[4,64,256]{2,1,0:T(8,128)S(1)} all-to-all(f32[4,64,256]{2,1,0:T(8,128)S(1)} %pad_maximum_fusion.1), channel_id=1, replica_groups=mesh['gx'=8,'gy'=4] {'gy'}, dimensions={0} | all-to-all | bytes 524288 | tf_op jit(solution)/shard_map/all_to_all | solution.py:170
  849.5 3.6 all-to-all-start.5
  854.3 10.7 %all-to-all-done.5 = f32[8,32,320]{2,1,0:T(8,128)S(1)} async-done(((f32[8,32,320]{2,1,0:T(8,128)}), f32[8,32,320]{2,1,0:T(8,128)S(1)}, u32[]{:S(2)}, u32[]{:S(2)}) %all-to-all-start.5) | async-done | bytes 327712 | tf_op jit(solution)/shard_map/all_to_all | solution.py:173
  874.7 8.7 convolution_bitcast_fusion.1
  883.5 6.9 copy.909
  890.4 6.4 reshape.2054
  896.8 51.8 %all_to_all.120 = f32[32,8,2048]{2,0,1:T(8,128)} all-to-all(f32[32,8,2048]{2,0,1:T(8,128)S(1)} %reshape.2054), channel_id=1, replica_groups=mesh['gx'=8,'gy'=4] {'gx'}, dimensions={1} | all-to-all | bytes 4194304 | tf_op jit(solution)/shard_map/all_to_all | solution.py:176
  948.6 6.2 reshape.1207
  954.8 7.0 copy.887
  961.8 7.0 fusion.1204
  971.6 29.2 %all_to_all.121 = f32[64,4,2048]{2,0,1:T(8,128)} all-to-all(f32[64,4,2048]{2,0,1:T(8,128)S(1)} %copy.888), channel_id=1, replica_groups=mesh['gx'=8,'gy'=4] {'gy'}, dimensions={1} | all-to-all | bytes 4194304 | tf_op jit(solution)/shard_map/all_to_all | solution.py:179
  1000.8 5.0 reshape.1208
  1005.8 14.0 %multiply_reduce_fusion.1 = (f32[]{:T(128)}, f32[]{:T(128)}, f32[32,64,256]{2,1,0:T(8,128)}) fusion(f32[32,64,256]{2,1,0:T(8,128)} %param.834, f32[32,64,256]{2,1,0:T(8,128)S(1)} %copy-done.1, s32[256]{0:T(256)S(1)} %copy-done.95, f32[256,32,64]{2,1,0:T(8,128)} %reshape.1208), kind=kOutput, calls=%fused_computation.1798 | convolution fusion | flops 1613299712 | bytes 8389640 | tf_op jit(solution)/shard_map/kab,kz->abz/dot_general | solution.py:159
  1021.1 40.1 %all-reduce = (f32[1]{0:T(128)}, f32[1]{0:T(128)}) all-reduce(f32[1]{0:T(128)} %bitcast.1856, f32[1]{0:T(128)} %bitcast.1855), channel_id=1, replica_groups=mesh['gx'=8,'gy'=4] {'gx','gy'}, use_global_device_ids=true, to_apply=%region_23.24 | all-reduce | flops 2 | bytes 16 | tf_op jit(solution)/shard_map/psum | solution.py:318
  (1316 shorter events, 373.3 us)
Async XLA Ops:
  0.6 275.2 %copy-start.94 = (s32[256]{0:T(256)}, s32[256]{0:T(256)S(1)}, u32[]{:S(2)}) copy-start(s32[256]{0:T(256)S(1)} %iota_add_fusion) | copy-start | bytes 3076
  13.0 29.9 %all-to-all-start = ((f32[4,64,2048]{2,1,0:T(8,128)}), f32[4,64,2048]{2,1,0:T(8,128)S(1)}, u32[]{:S(2)}, u32[]{:S(2)}) async-start(f32[4,64,2048]{2,1,0:T(8,128)} %copy.900), calls=%async_computation | async-start | bytes 4194304 | tf_op jit(solution)/shard_map/all_to_all | solution.py:170
  17.2 28.7 %copy-start.565 = (s32[64,4]{0,1:T(4,128)}, s32[64,4]{0,1:T(4,128)S(1)}, u32[]{:S(2)}) copy-start(s32[64,4]{0,1:T(4,128)S(1)} %add_add_fusion.8) | copy-start | bytes 3076
  17.2 120.4 %copy-start.489 = (s32[8,32]{1,0:T(8,128)}, s32[8,32]{1,0:T(8,128)S(1)}, u32[]{:S(2)}) copy-start(s32[8,32]{1,0:T(8,128)S(1)} %add_add_fusion.7) | copy-start | bytes 3076
  55.1 66.2 %all-to-all-start.1 = ((f32[8,32,2048]{2,1,0:T(8,128)}), f32[8,32,2048]{2,1,0:T(8,128)S(1)}, u32[]{:S(2)}, u32[]{:S(2)}) async-start(f32[8,32,2048]{2,1,0:T(8,128)} %convolution_bitcast_fusion), calls=%async_computation.1 | async-start | bytes 4194304 | tf_op jit(solution)/shard_map/all_to_all | solution.py:173
  62.2 63.9 %copy-start.567 = (f32[256]{0:T(256)}, f32[256]{0:T(256)S(1)}, u32[]{:S(2)}) copy-start(f32[256]{0:T(256)S(1)} %multiply_multiply_fusion.64) | copy-start | bytes 3076
  62.3 63.8 %copy-start.467 = (f32[32,64]{1,0:T(8,128)}, f32[32,64]{1,0:T(8,128)S(1)}, u32[]{:S(2)}) copy-start(f32[32,64]{1,0:T(8,128)S(1)} %broadcast_add_fusion) | copy-start | bytes 24580
  160.5 52.0 %all-to-all-start.2 = ((f32[32,8,2048]{2,0,1:T(8,128)}), f32[32,8,2048]{2,0,1:T(8,128)S(1)}, u32[]{:S(2)}, u32[]{:S(2)}) async-start(f32[32,8,2048]{2,0,1:T(8,128)} %reshape.2047), calls=%async_computation.2 | async-start | bytes 4194304 | tf_op jit(solution)/shard_map/all_to_all | solution.py:176
  164.3 60.0 %copy-start.497 = (s32[4,64]{1,0:T(4,128)}, s32[4,64]{1,0:T(4,128)S(1)}, u32[]{:S(2)}) copy-start(s32[4,64]{1,0:T(4,128)S(1)} %add_add_fusion.9) | copy-start | bytes 3076
  235.1 29.2 %all-to-all-start.3 = ((f32[64,4,2048]{2,0,1:T(8,128)}), f32[64,4,2048]{2,0,1:T(8,128)S(1)}, u32[]{:S(2)}, u32[]{:S(2)}) async-start(f32[64,4,2048]{2,0,1:T(8,128)} %copy.873), calls=%async_computation.3 | async-start | bytes 4194304 | tf_op jit(solution)/shard_map/all_to_all | solution.py:179
  240.1 143.1 %copy-start.4 = (f32[8,2,8,128]{3,1,2,0:T(2,128)}, f32[8,2,8,128]{3,1,2,0:T(2,128)S(1)}, u32[]{:S(2)}) copy-start(f32[8,2,8,128]{3,1,2,0:T(2,128)S(1)} %copy.915) | copy-start | bytes 196612
  241.0 88.3 %copy-start.407 = (f32[2048]{0:T(1024)}, f32[2048]{0:T(1024)S(1)}, u32[]{:S(2)}) copy-start(f32[2048]{0:T(1024)S(1)} %get-tuple-element.2775) | copy-start | bytes 24580
  241.0 92.1 %copy-start.405 = (f32[2048]{0:T(1024)}, f32[2048]{0:T(1024)S(1)}, u32[]{:S(2)}) copy-start(f32[2048]{0:T(1024)S(1)} %get-tuple-element.2776) | copy-start | bytes 24580
  241.0 88.2 %copy-start.453 = (f32[2048]{0:T(1024)}, f32[2048]{0:T(1024)S(1)}, u32[]{:S(2)}) copy-start(f32[2048]{0:T(1024)S(1)} %get-tuple-element.3227) | copy-start | bytes 24580
  241.1 88.2 %copy-start.455 = (f32[2048]{0:T(1024)}, f32[2048]{0:T(1024)S(1)}, u32[]{:S(2)}) copy-start(f32[2048]{0:T(1024)S(1)} %get-tuple-element.3225) | copy-start | bytes 24580
  241.1 88.2 %copy-start.457 = (f32[2048]{0:T(1024)}, f32[2048]{0:T(1024)S(1)}, u32[]{:S(2)}) copy-start(f32[2048]{0:T(1024)S(1)} %get-tuple-element.3223) | copy-start | bytes 24580
  241.1 88.2 %copy-start.459 = (f32[2048]{0:T(1024)}, f32[2048]{0:T(1024)S(1)}, u32[]{:S(2)}) copy-start(f32[2048]{0:T(1024)S(1)} %get-tuple-element.3221) | copy-start | bytes 24580
  241.1 88.2 %copy-start.461 = (f32[2048]{0:T(1024)}, f32[2048]{0:T(1024)S(1)}, u32[]{:S(2)}) copy-start(f32[2048]{0:T(1024)S(1)} %get-tuple-element.3219) | copy-start | bytes 24580
  241.1 92.0 %copy-start.443 = (f32[2048]{0:T(1024)}, f32[2048]{0:T(1024)S(1)}, u32[]{:S(2)}) copy-start(f32[2048]{0:T(1024)S(1)} %get-tuple-element.3228) | copy-start | bytes 24580
  241.1 92.0 %copy-start.445 = (f32[2048]{0:T(1024)}, f32[2048]{0:T(1024)S(1)}, u32[]{:S(2)}) copy-start(f32[2048]{0:T(1024)S(1)} %get-tuple-element.3226) | copy-start | bytes 24580
  241.1 92.0 %copy-start.447 = (f32[2048]{0:T(1024)}, f32[2048]{0:T(1024)S(1)}, u32[]{:S(2)}) copy-start(f32[2048]{0:T(1024)S(1)} %get-tuple-element.3224) | copy-start | bytes 24580
  241.1 92.0 %copy-start.449 = (f32[2048]{0:T(1024)}, f32[2048]{0:T(1024)S(1)}, u32[]{:S(2)}) copy-start(f32[2048]{0:T(1024)S(1)} %get-tuple-element.3222) | copy-start | bytes 24580
  241.1 92.0 %copy-start.451 = (f32[2048]{0:T(1024)}, f32[2048]{0:T(1024)S(1)}, u32[]{:S(2)}) copy-start(f32[2048]{0:T(1024)S(1)} %get-tuple-element.3220) | copy-start | bytes 24580
  287.2 226.4 %copy-start = (f32[32,64,256]{2,1,0:T(8,128)}, f32[32,64,256]{2,1,0:T(8,128)S(1)}, u32[]{:S(2)}) copy-start(f32[32,64,256]{2,1,0:T(8,128)S(1)} %fusion.1202) | copy-start | bytes 6291460
  289.3 42.0 %copy-start.463 = (f32[2048]{0:T(1024)}, f32[2048]{0:T(1024)S(1)}, u32[]{:S(2)}) copy-start(f32[2048]{0:T(1024)S(1)} %get-tuple-element.3265) | copy-start | bytes 24580
  289.3 42.0 %copy-start.465 = (f32[2048]{0:T(1024)}, f32[2048]{0:T(1024)S(1)}, u32[]{:S(2)}) copy-start(f32[2048]{0:T(1024)S(1)} %get-tuple-element.3267) | copy-start | bytes 24580
  331.2 25.9 %copy-start.9 = (f32[17,2048]{1,0:T(8,128)}, f32[17,2048]{1,0:T(8,128)S(1)}, u32[]{:S(2)}) copy-start(f32[17,2048]{1,0:T(8,128)S(1)} %get-tuple-element.2772) | copy-start | bytes 417796
  331.2 27.6 %copy-start.11 = (f32[17,2048]{1,0:T(8,128)}, f32[17,2048]{1,0:T(8,128)S(1)}, u32[]{:S(2)}) copy-start(f32[17,2048]{1,0:T(8,128)S(1)} %get-tuple-element.2771) | copy-start | bytes 417796
  331.2 29.8 %copy-start.13 = (f32[17,2048]{1,0:T(8,128)}, f32[17,2048]{1,0:T(8,128)S(1)}, u32[]{:S(2)}) copy-start(f32[17,2048]{1,0:T(8,128)S(1)} %get-tuple-element.2770) | copy-start | bytes 417796
  331.3 31.5 %copy-start.15 = (f32[17,2048]{1,0:T(8,128)}, f32[17,2048]{1,0:T(8,128)S(1)}, u32[]{:S(2)}) copy-start(f32[17,2048]{1,0:T(8,128)S(1)} %get-tuple-element.2769) | copy-start | bytes 417796
  331.3 33.1 %copy-start.17 = (f32[17,2048]{1,0:T(8,128)}, f32[17,2048]{1,0:T(8,128)S(1)}, u32[]{:S(2)}) copy-start(f32[17,2048]{1,0:T(8,128)S(1)} %get-tuple-element.2768) | copy-start | bytes 417796
  331.3 34.8 %copy-start.19 = (f32[17,2048]{1,0:T(8,128)}, f32[17,2048]{1,0:T(8,128)S(1)}, u32[]{:S(2)}) copy-start(f32[17,2048]{1,0:T(8,128)S(1)} %get-tuple-element.2767) | copy-start | bytes 417796
  331.3 36.5 %copy-start.21 = (f32[17,2048]{1,0:T(8,128)}, f32[17,2048]{1,0:T(8,128)S(1)}, u32[]{:S(2)}) copy-start(f32[17,2048]{1,0:T(8,128)S(1)} %get-tuple-element.2766) | copy-start | bytes 417796
  331.3 38.2 %copy-start.23 = (f32[17,2048]{1,0:T(8,128)}, f32[17,2048]{1,0:T(8,128)S(1)}, u32[]{:S(2)}) copy-start(f32[17,2048]{1,0:T(8,128)S(1)} %get-tuple-element.2765) | copy-start | bytes 417796
  331.3 39.9 %copy-start.27 = (f32[17,2048]{1,0:T(8,128)}, f32[17,2048]{1,0:T(8,128)S(1)}, u32[]{:S(2)}) copy-start(f32[17,2048]{1,0:T(8,128)S(1)} %get-tuple-element.2764) | copy-start | bytes 417796
  335.1 26.8 %copy-start.53 = (f32[17,2048]{1,0:T(8,128)}, f32[17,2048]{1,0:T(8,128)S(1)}, u32[]{:S(2)}) copy-start(f32[17,2048]{1,0:T(8,128)S(1)} %get-tuple-element.2800) | copy-start | bytes 417796
  335.1 28.5 %copy-start.55 = (f32[17,2048]{1,0:T(8,128)}, f32[17,2048]{1,0:T(8,128)S(1)}, u32[]{:S(2)}) copy-start(f32[17,2048]{1,0:T(8,128)S(1)} %get-tuple-element.2799) | copy-start | bytes 417796
  335.1 30.2 %copy-start.57 = (f32[17,2048]{1,0:T(8,128)}, f32[17,2048]{1,0:T(8,128)S(1)}, u32[]{:S(2)}) copy-start(f32[17,2048]{1,0:T(8,128)S(1)} %get-tuple-element.2798) | copy-start | bytes 417796
  335.1 31.9 %copy-start.59 = (f32[17,2048]{1,0:T(8,128)}, f32[17,2048]{1,0:T(8,128)S(1)}, u32[]{:S(2)}) copy-start(f32[17,2048]{1,0:T(8,128)S(1)} %get-tuple-element.2797) | copy-start | bytes 417796
  335.1 33.5 %copy-start.61 = (f32[17,2048]{1,0:T(8,128)}, f32[17,2048]{1,0:T(8,128)S(1)}, u32[]{:S(2)}) copy-start(f32[17,2048]{1,0:T(8,128)S(1)} %get-tuple-element.2796) | copy-start | bytes 417796
  335.1 35.2 %copy-start.63 = (f32[17,2048]{1,0:T(8,128)}, f32[17,2048]{1,0:T(8,128)S(1)}, u32[]{:S(2)}) copy-start(f32[17,2048]{1,0:T(8,128)S(1)} %get-tuple-element.2795) | copy-start | bytes 417796
  335.1 36.9 %copy-start.67 = (f32[17,2048]{1,0:T(8,128)}, f32[17,2048]{1,0:T(8,128)S(1)}, u32[]{:S(2)}) copy-start(f32[17,2048]{1,0:T(8,128)S(1)} %get-tuple-element.2794) | copy-start | bytes 417796
  383.2 113.2 %copy-start.6 = (f32[4,2,8,128]{3,1,2,0:T(2,128)S(1)}, f32[4,2,8,128]{3,1,2,0:T(2,128)}, u32[]{:S(2)}) copy-start(f32[4,2,8,128]{3,1,2,0:T(2,128)} %copy.917) | copy-start | bytes 98308
  383.3 113.2 %copy-start.78 = (f32[4,2,8,128]{3,1,2,0:T(2,128)S(1)}, f32[4,2,8,128]{3,1,2,0:T(2,128)}, u32[]{:S(2)}) copy-start(f32[4,2,8,128]{3,1,2,0:T(2,128)} %copy.916) | copy-start | bytes 98308
  383.4 54.9 %copy-start.570 = (f32[17]{0:T(128)}, f32[17]{0:T(128)S(1)}, u32[]{:S(2)}) copy-start(f32[17]{0:T(128)S(1)} %multiply_bitcast_fusion.4) | copy-start | bytes 208 | tf_op jit(solution)/shard_map/cond
  383.4 49.8 %copy-start.564 = (f32[17]{0:T(128)}, f32[17]{0:T(128)S(1)}, u32[]{:S(2)}) copy-start(f32[17]{0:T(128)S(1)} %get-tuple-element.2867) | copy-start | bytes 208 | tf_op jit(solution)/shard_map/cond
  385.1 62.1 %copy-start.471 = (f32[16384]{0:T(1024)}, f32[16384]{0:T(1024)S(1)}, u32[]{:S(2)}) copy-start(f32[16384]{0:T(1024)S(1)} %get-tuple-element.2621) | copy-start | bytes 196612 | tf_op jit(solution)/shard_map/cond
  386.2 40.6 %copy-start.86 = (f32[16384]{0:T(1024)}, f32[16384]{0:T(1024)S(1)}, u32[]{:S(2)}) copy-start(f32[16384]{0:T(1024)S(1)} %get-tuple-element.2828) | copy-start | bytes 196612 | tf_op jit(solution)/shard_map/cond
  386.2 47.0 %copy-start.88 = (f32[16384]{0:T(1024)}, f32[16384]{0:T(1024)S(1)}, u32[]{:S(2)}) copy-start(f32[16384]{0:T(1024)S(1)} %get-tuple-element.2830) | copy-start | bytes 196612 | tf_op jit(solution)/shard_map/cond
  386.2 47.0 %copy-start.90 = (f32[16384]{0:T(1024)}, f32[16384]{0:T(1024)S(1)}, u32[]{:S(2)}) copy-start(f32[16384]{0:T(1024)S(1)} %get-tuple-element.2832) | copy-start | bytes 196612 | tf_op jit(solution)/shard_map/cond
  386.2 64.1 %copy-start.477 = (f32[16384]{0:T(1024)}, f32[16384]{0:T(1024)S(1)}, u32[]{:S(2)}) copy-start(f32[16384]{0:T(1024)S(1)} %get-tuple-element.2862) | copy-start | bytes 196612 | tf_op jit(solution)/shard_map/cond
  568.5 57.7 %copy-start.74 = (f32[17,2048]{1,0:T(8,128)S(1)}, f32[17,2048]{1,0:T(8,128)}, u32[]{:S(2)}) copy-start(f32[17,2048]{1,0:T(8,128)} %copy-done.73) | copy-start | bytes 417796
  568.5 57.9 %copy-start.72 = (f32[17,2048]{1,0:T(8,128)S(1)}, f32[17,2048]{1,0:T(8,128)}, u32[]{:S(2)}) copy-start(f32[17,2048]{1,0:T(8,128)} %copy-done.71) | copy-start | bytes 417796
  568.5 58.1 %copy-start.70 = (f32[17,2048]{1,0:T(8,128)S(1)}, f32[17,2048]{1,0:T(8,128)}, u32[]{:S(2)}) copy-start(f32[17,2048]{1,0:T(8,128)} %copy-done.69) | copy-start | bytes 417796
  568.5 58.3 %copy-start.66 = (f32[17,2048]{1,0:T(8,128)S(1)}, f32[17,2048]{1,0:T(8,128)}, u32[]{:S(2)}) copy-start(f32[17,2048]{1,0:T(8,128)} %copy-done.65) | copy-start | bytes 417796
  568.5 58.6 %copy-start.68 = (f32[17,2048]{1,0:T(8,128)S(1)}, f32[17,2048]{1,0:T(8,128)}, u32[]{:S(2)}) copy-start(f32[17,2048]{1,0:T(8,128)} %copy-done.67) | copy-start | bytes 417796
  568.5 58.8 %copy-start.64 = (f32[17,2048]{1,0:T(8,128)S(1)}, f32[17,2048]{1,0:T(8,128)}, u32[]{:S(2)}) copy-start(f32[17,2048]{1,0:T(8,128)} %copy-done.63) | copy-start | bytes 417796
  568.5 59.0 %copy-start.62 = (f32[17,2048]{1,0:T(8,128)S(1)}, f32[17,2048]{1,0:T(8,128)}, u32[]{:S(2)}) copy-start(f32[17,2048]{1,0:T(8,128)} %copy-done.61) | copy-start | bytes 417796
  568.5 59.3 %copy-start.60 = (f32[17,2048]{1,0:T(8,128)S(1)}, f32[17,2048]{1,0:T(8,128)}, u32[]{:S(2)}) copy-start(f32[17,2048]{1,0:T(8,128)} %copy-done.59) | copy-start | bytes 417796
  577.0 51.1 %copy-start.58 = (f32[17,2048]{1,0:T(8,128)S(1)}, f32[17,2048]{1,0:T(8,128)}, u32[]{:S(2)}) copy-start(f32[17,2048]{1,0:T(8,128)} %copy-done.57) | copy-start | bytes 417796
  668.0 49.7 %copy-start.5 = (f32[8,2,8,128]{3,1,2,0:T(2,128)S(1)}, f32[8,2,8,128]{3,1,2,0:T(2,128)}, u32[]{:S(2)}) copy-start(f32[8,2,8,128]{3,1,2,0:T(2,128)} %copy-done.4) | copy-start | bytes 196612
  734.0 82.0 %copy-start.95 = (s32[256]{0:T(256)S(1)}, s32[256]{0:T(256)}, u32[]{:S(2)}) copy-start(s32[256]{0:T(256)} %copy-done.94) | copy-start | bytes 3076
  820.1 26.7 %copy-start.498 = (s32[4,64]{1,0:T(4,128)S(1)}, s32[4,64]{1,0:T(4,128)}, u32[]{:S(2)}) copy-start(s32[4,64]{1,0:T(4,128)} %copy-done.497) | copy-start | bytes 3076
  849.5 15.4 %all-to-all-start.5 = ((f32[8,32,320]{2,1,0:T(8,128)}), f32[8,32,320]{2,1,0:T(8,128)S(1)}, u32[]{:S(2)}, u32[]{:S(2)}) async-start(f32[8,32,320]{2,1,0:T(8,128)} %pad_maximum_fusion), calls=%async_computation.5 | async-start | bytes 786432 | tf_op jit(solution)/shard_map/all_to_all | solution.py:173
  (404 other events, 2278.3 us)
where the time goes:
time: 1080 us; the launch traced here: 1060 us
  matrix products  440 us (41%)
  blocking collectives  185 us (17%)
  waiting for transfers between devices  167 us (15%)
  local copies, waits for them, and re-layouts  122 us (11%)
  loops' own time  62.3 us (6%)
  other arithmetic  59.1 us (5%)
  starting transfers between devices  22 us (2%)
    dot_general x68, matrix products, visitor(): jnp.dot(sine_now, weight, precision=exact_mode)  105 us
    dot_general x68, matrix products, visitor(): jnp.dot(cosine_now, weight, precision=exact_mode)  102 us
    dot_general x68, matrix products, visitor(): jnp.dot(weight_cosine[degree], cosine_now, precision=exact_mode)  71.4 us
    all_to_all x2, waiting for transfers between devices, swap_two(): lax.all_to_all(operand, 'gx', split_axis=0, concat_axis=1, tiled=True)  69.7 us
    dot_general x68, matrix products, visitor(): return accum + jnp.dot(weight_sine[degree], sine_now, precision=exact_mode)  65.3 us
    all_to_all x1, blocking collectives, back_two(): lax.all_to_all(operand, 'gx', split_axis=1, concat_axis=0, tiled=True)  51.8 us
    all_to_all x1, waiting for transfers between devices, back_two(): lax.all_to_all(operand, 'gx', split_axis=1, concat_axis=0, tiled=True)  48.2 us
    psum x1, blocking collectives, shards(): sum_cosine, sum_sine = lax.psum((mom_cosine, mom_sine), ('gx', 'gy'))  40.4 us
  transfers between devices with their start and end apart: 5, of which 5 were waited for; matrix products, arithmetic and copies ran while one was open for 0% of the time, Pallas kernels for 0%

commit v1 on v0

--- a/solution.py
+++ b/solution.py
@@ -176,7 +176,10 @@
         return lax.all_to_all(operand, "gx", split_axis=1, concat_axis=0, tiled=True)
 
     def back_one(operand):
-        return lax.all_to_all(operand, "gy", split_axis=1, concat_axis=0, tiled=True)
+        return jnp.concatenate(
+            lax.all_to_all(jnp.stack(jnp.split(operand, lax.axis_size("gy"), axis=1)), "gy", 0, 0),
+            axis=0,
+        )
 
     groups_one = lax.axis_size("gy")
     groups_two = lax.axis_size("gx")

time: 1080 us -> 1070 us (level)
  waiting for transfers between devices: 167 us -> 155 us
    reshape x2 -> x0, local copies, waits for them, and re-layouts: 16.5 us -> none  [inverse(): volume = volume.reshape(length, cells_a, cells_b)]
    unnamed x498 -> x518, local copies, waits for them, and re-layouts: 6.51 us -> 17.8 us
    all_to_all x2, waiting for transfers between devices: 69.7 us -> 58.5 us  [swap_two(): lax.all_to_all(operand, 'gx', split_axis=0, concat_axis=1, tiled=True)]
where the time goes in v1:
time: 1070 us; the launch traced here: 1060 us
  matrix products  435 us (41%)
  blocking collectives  193 us (18%)
  waiting for transfers between devices  155 us (14%)
  local copies, waits for them, and re-layouts  121 us (11%)
  loops' own time  62.3 us (6%)
  other arithmetic  60.7 us (6%)
  starting transfers between devices  22.4 us (2%)
    dot_general x68, matrix products, visitor(): jnp.dot(sine_now, weight, precision=exact_mode)  105 us
    dot_general x68, matrix products, visitor(): jnp.dot(cosine_now, weight, precision=exact_mode)  102 us
    dot_general x68, matrix products, visitor(): jnp.dot(weight_cosine[degree], cosine_now, precision=exact_mode)  71.4 us
    dot_general x68, matrix products, visitor(): return accum + jnp.dot(weight_sine[degree], sine_now, precision=exact_mode)  65.3 us
    all_to_all x2, waiting for transfers between devices, swap_two(): lax.all_to_all(operand, 'gx', split_axis=0, concat_axis=1, tiled=True)  58.5 us
    all_to_all x1, blocking collectives, back_two(): lax.all_to_all(operand, 'gx', split_axis=1, concat_axis=0, tiled=True)  51.5 us
    all_to_all x1, waiting for transfers between devices, back_two(): lax.all_to_all(operand, 'gx', split_axis=1, concat_axis=0, tiled=True)  47.9 us
    psum x1, blocking collectives, shards(): sum_cosine, sum_sine = lax.psum((mom_cosine, mom_sine), ('gx', 'gy'))  47.8 us
  transfers between devices with their start and end apart: 5, of which 5 were waited for; matrix products, arithmetic and copies ran while one was open for 0% of the time, Pallas kernels for 0%

profile of v1, /device:TPU:0, one launch (start us, length us, event | category | flops | bytes accessed | tf_op | source)
XLA Modules:
  0.0 1055.8 jit_solution(10771726672896726292)
XLA Ops:
  0.6 4.5 fusion.1266
  8.2 4.7 copy.918
  13.0 4.2 all-to-all-start
  17.3 25.6 %all-to-all-done = f32[4,64,2048]{2,1,0:T(8,128)S(1)} async-done(((f32[4,64,2048]{2,1,0:T(8,128)}), f32[4,64,2048]{2,1,0:T(8,128)S(1)}, u32[]{:S(2)}, u32[]{:S(2)}) %all-to-all-start) | async-done | bytes 2097184 | tf_op jit(solution)/shard_map/all_to_all | solution.py:170
  45.9 9.2 convolution_bitcast_fusion
  55.1 6.9 all-to-all-start.1
  62.2 48.0 %all-to-all-done.1 = f32[8,32,2048]{2,1,0:T(8,128)S(1)} async-done(((f32[8,32,2048]{2,1,0:T(8,128)}), f32[8,32,2048]{2,1,0:T(8,128)S(1)}, u32[]{:S(2)}, u32[]{:S(2)}) %all-to-all-start.1) | async-done | bytes 2097184 | tf_op jit(solution)/shard_map/all_to_all | solution.py:173
  110.3 4.8 reshape.2034
  115.0 11.5 %bitcast_divide_fusion = f32[32,64,256]{2,1,0:T(8,128)S(1)} fusion(f32[32,8,64,32]{3,2,0,1:T(8,128)} %reshape.2034, f32[256]{0:T(256)S(1)} %multiply_multiply_fusion.64, f32[32,64]{1,0:T(8,128)S(1)} %broadcast_add_fusion, s32[256]{0:T(256)S(1)} %iota_add_fusion, s32[8,32]{1,0:T(8,128)S(1)} %add_add_fusion.7), kind=kOutput, calls=%fused_computation.1785 | convolution fusion | flops 1612775424 | bytes 4205568 | tf_op jit(solution)/shard_map/kqzc,qcj->kzj/dot_general | solution.py:144
  127.9 7.0 convolution_bitcast_fusion.2
  135.0 6.9 copy.923
  141.9 7.5 reshape.2035
  149.4 4.0 all-to-all-start.2
  153.6 47.9 %all-to-all-done.2 = f32[32,8,2048]{2,0,1:T(8,128)S(1)} async-done(((f32[32,8,2048]{2,0,1:T(8,128)}), f32[32,8,2048]{2,0,1:T(8,128)S(1)}, u32[]{:S(2)}, u32[]{:S(2)}) %all-to-all-start.2) | async-done | bytes 2097184 | tf_op jit(solution)/shard_map/all_to_all | solution.py:176
  201.5 4.8 reshape.1185
  206.3 7.0 copy.884
  213.3 4.6 fusion.1211
  226.2 3.6 all-to-all-start.3
  232.3 23.1 %all-to-all-done.3 = f32[4,64,2048]{2,1,0:T(8,128)S(1)} async-done(((f32[4,64,2048]{2,1,0:T(8,128)}), f32[4,64,2048]{2,1,0:T(8,128)S(1)}, u32[]{:S(2)}, u32[]{:S(2)}) %all-to-all-start.3) | async-done | bytes 2097184 | tf_op jit(solution)/shard_map/all_to_all | solution.py:180
  255.5 3.2 reshape_reshape.6
  258.7 11.3 %fusion.1202 = f32[32,64,256]{2,1,0:T(8,128)S(1)} fusion(f32[256,32,64]{2,1,0:T(8,128)} %reshape_reshape.6, s32[256]{0:T(256)S(1)} %iota_add_fusion), kind=kOutput, calls=%fused_computation.1780 | convolution fusion | flops 1611202560 | bytes 4195328 | tf_op jit(solution)/shard_map/kab,kz->abz/dot_general | solution.py:159
  356.1 10.0 conditional.9
  366.1 113.1 %conditional.8 = (f32[17,17]{1,0:T(8,128)S(1)}, f32[17,17]{1,0:T(8,128)S(1)}) conditional(s32[]{:T(128)} %convert_element_type.118, () %tuple.64, (f32[17,1]{0,1:T(1,128)S(1)}, f32[16384]{0:T(1024)}, f32[16384]{0:T(1024)S(1)}, f32[16384]{0:T(1024)S(1)}, f32[17,1]{0,1:T(1,128)S(1)}, /*index=5*/f32[17,1]{0,1:T(1,128)S(1)}, ...), branch_computations={%region_0.1_spmd, %region_1.2_spmd} | conditional | flops 290816064 | bytes 57925084 | solution.py:233
  374.4 4.6 fusion.115
  379.0 4.5 fusion.114
  383.5 4.3 fusion.113
  387.7 4.1 fusion.112
  391.9 3.8 fusion.109
  395.6 3.9 fusion.108
  399.6 3.4 fusion.107
  403.0 3.5 fusion.106
  412.7 3.2 fusion.77
  423.6 6.4 multiply_add_fusion.2
  451.0 3.9 stack.501
  454.9 7.8 multiply_add_fusion.17
  479.9 16.6 %conditional.11 = (f32[17,17]{1,0:T(8,128)S(1)}, f32[17,17]{1,0:T(8,128)S(1)}) conditional(s32[]{:T(128)} %convert_element_type.121, () %tuple.69, (f32[17,1]{0,1:T(1,128)S(1)}, f32[8192]{0:T(1024)S(1)}, f32[8192]{0:T(1024)S(1)}, f32[8192]{0:T(1024)S(1)}, f32[17,1]{0,1:T(1,128)S(1)}, /*index=5*/f32[17,1]{0,1:T(1,128)S(1)}, ...), branch_computations={%region_6.7_spmd, %region_7.8_spmd} | conditional | flops 145408080 | bytes 28004404 | solution.py:233
  497.0 54.3 %conditional.10 = (f32[17,17]{1,0:T(8,128)}, f32[17,17]{1,0:T(8,128)}) conditional(s32[]{:T(128)} %convert_element_type.120, () %tuple.67, (f32[17,1]{0,1:T(1,128)S(1)}, f32[8192]{0:T(1024)S(1)}, f32[8192]{0:T(1024)S(1)}, f32[8192]{0:T(1024)S(1)}, f32[17,1]{0,1:T(1,128)S(1)}, /*index=5*/f32[17,1]{0,1:T(1,128)S(1)}, f32[32,64,256]{2,1,0:T(8,128)S(1)}, ...), branch_computations={%region_4.5_spmd, %region_5.6_spmd} | conditional | flops 145408080 | bytes 27208952 | solution.py:233
  560.6 47.8 %all-reduce.1 = (f32[17,17]{1,0:T(8,128)S(1)}, f32[17,17]{1,0:T(8,128)S(1)}) all-reduce(f32[17,17]{1,0:T(8,128)S(1)} %get-tuple-element.3289, f32[17,17]{1,0:T(8,128)S(1)} %get-tuple-element.3288), channel_id=1, replica_groups=mesh['gx'=8,'gy'=4] {'gx','gy'}, use_global_device_ids=true, to_apply=%region_8.9 | all-reduce | flops 578 | bytes 4624 | tf_op jit(solution)/shard_map/psum | solution.py:239
  648.2 10.0 conditional.13
  658.8 48.3 %conditional.12 = (f32[8192]{0:T(1024)S(1)}) conditional(s32[]{:T(128)} %convert_element_type.120, () %tuple.70, (f32[17,1]{0,1:T(1,128)S(1)}, f32[8192]{0:T(1024)S(1)}, f32[8192]{0:T(1024)S(1)}, f32[8192]{0:T(1024)S(1)}, f32[17,1]{0,1:T(1,128)S(1)}, /*index=5*/f32[17,1]{0,1:T(1,128)S(1)}, f32[17,17]{1,0:T(8,128)S(1)}, f32[17,1]{0,1:T(1,128)S(1)}, ...), branch_computations={%region_10.11_spmd, %region_11.12_spmd} | conditional | flops 145293392 | bytes 33228644 | solution.py:249
  708.5 15.7 %conditional.15 = (f32[16384]{0:T(1024)S(1)}) conditional(s32[]{:T(128)} %convert_element_type.119, () %tuple.75, (f32[17,1]{0,1:T(1,128)S(1)}, f32[16384]{0:T(1024)}, f32[16384]{0:T(1024)S(1)}, f32[16384]{0:T(1024)S(1)}, f32[17,1]{0,1:T(1,128)S(1)}, /*index=5*/f32[17,1]{0,1:T(1,128)S(1)}, f32[17,17]{1,0:T(8,128)S(1)}, f32[17,1]{0,1:T(1,128)S(1)}, ...), branch_computations={%region_16.17_spmd, %region_17.18_spmd} | conditional | flops 290586688 | bytes 66294256 | solution.py:249
  724.3 81.9 %conditional.14 = (f32[16384]{0:T(1024)S(1)}) conditional(s32[]{:T(128)} %convert_element_type.118, () %tuple.73, (f32[17,1]{0,1:T(1,128)S(1)}, f32[16384]{0:T(1024)}, f32[16384]{0:T(1024)S(1)}, f32[16384]{0:T(1024)S(1)}, f32[17,1]{0,1:T(1,128)S(1)}, /*index=5*/f32[17,1]{0,1:T(1,128)S(1)}, f32[17,17]{1,0:T(8,128)S(1)}, f32[17,1]{0,1:T(1,128)S(1)}, ...), branch_computations={%region_14.15_spmd, %region_15.16_spmd} | conditional | flops 290586688 | bytes 66291856 | solution.py:249
  728.9 3.9 fusion.948
  732.8 3.8 fusion.950
  736.6 3.6 fusion.952
  740.3 3.4 fusion.954
  743.7 3.1 fusion.956
  749.6 3.5 fusion.958
  768.4 6.4 multiply_add_fusion.334
  787.0 6.5 multiply_add_fusion.335
  810.5 24.3 %all_to_all.97 = f32[4,64,256]{2,1,0:T(8,128)S(1)} all-to-all(f32[4,64,256]{2,1,0:T(8,128)S(1)} %pad_maximum_fusion.3), channel_id=1, replica_groups=mesh['gx'=8,'gy'=4] {'gy'}, dimensions={0} | all-to-all | bytes 524288 | tf_op jit(solution)/shard_map/all_to_all | solution.py:170
  840.5 3.6 all-to-all-start.5
  845.2 10.5 all-to-all-done.5
  865.5 8.7 convolution_bitcast_fusion.1
  874.2 6.9 copy.927
  881.1 6.4 reshape.2042
  887.6 51.5 %all_to_all.98 = f32[32,8,2048]{2,0,1:T(8,128)} all-to-all(f32[32,8,2048]{2,0,1:T(8,128)S(1)} %reshape.2042), channel_id=1, replica_groups=mesh['gx'=8,'gy'=4] {'gx'}, dimensions={1} | all-to-all | bytes 4194304 | tf_op jit(solution)/shard_map/all_to_all | solution.py:176
  939.1 6.2 reshape.1195
  945.3 7.0 copy.902
  952.3 4.5 fusion.1204
  964.1 29.2 %all_to_all.99 = f32[4,64,2048]{2,1,0:T(8,128)} all-to-all(f32[4,64,2048]{2,1,0:T(8,128)S(1)} %pad_maximum_fusion.1), channel_id=1, replica_groups=mesh['gx'=8,'gy'=4] {'gy'}, dimensions={0} | all-to-all | bytes 4194304 | tf_op jit(solution)/shard_map/all_to_all | solution.py:180
  993.2 5.0 reshape_reshape.7
  998.3 14.1 %multiply_reduce_fusion.1 = (f32[]{:T(128)}, f32[]{:T(128)}, f32[32,64,256]{2,1,0:T(8,128)}) fusion(f32[32,64,256]{2,1,0:T(8,128)} %param.834, f32[32,64,256]{2,1,0:T(8,128)S(1)} %copy-done.1, s32[256]{0:T(256)S(1)} %copy-done.101, f32[256,32,64]{2,1,0:T(8,128)} %reshape_reshape.7), kind=kOutput, calls=%fused_computation.1800 | convolution fusion | flops 1613299712 | bytes 8389640 | tf_op jit(solution)/shard_map/kab,kz->abz/dot_general | solution.py:159
  1013.6 39.9 %all-reduce = (f32[1]{0:T(128)}, f32[1]{0:T(128)}) all-reduce(f32[1]{0:T(128)} %bitcast.1864, f32[1]{0:T(128)} %bitcast.1863), channel_id=1, replica_groups=mesh['gx'=8,'gy'=4] {'gx','gy'}, use_global_device_ids=true, to_apply=%region_23.24 | all-reduce | flops 2 | bytes 16 | tf_op jit(solution)/shard_map/psum | solution.py:321
  (1338 shorter events, 382.8 us)
Async XLA Ops:
  0.6 258.0 %copy-start.100 = (s32[256]{0:T(256)}, s32[256]{0:T(256)S(1)}, u32[]{:S(2)}) copy-start(s32[256]{0:T(256)S(1)} %iota_add_fusion) | copy-start | bytes 3076
  13.0 29.9 %all-to-all-start = ((f32[4,64,2048]{2,1,0:T(8,128)}), f32[4,64,2048]{2,1,0:T(8,128)S(1)}, u32[]{:S(2)}, u32[]{:S(2)}) async-start(f32[4,64,2048]{2,1,0:T(8,128)} %copy.918), calls=%async_computation | async-start | bytes 4194304 | tf_op jit(solution)/shard_map/all_to_all | solution.py:170
  17.2 28.7 %copy-start.571 = (s32[64,4]{0,1:T(4,128)}, s32[64,4]{0,1:T(4,128)S(1)}, u32[]{:S(2)}) copy-start(s32[64,4]{0,1:T(4,128)S(1)} %add_add_fusion.8) | copy-start | bytes 3076
  17.3 109.3 %copy-start.495 = (s32[8,32]{1,0:T(8,128)}, s32[8,32]{1,0:T(8,128)S(1)}, u32[]{:S(2)}) copy-start(s32[8,32]{1,0:T(8,128)S(1)} %add_add_fusion.7) | copy-start | bytes 3076
  55.1 55.2 %all-to-all-start.1 = ((f32[8,32,2048]{2,1,0:T(8,128)}), f32[8,32,2048]{2,1,0:T(8,128)S(1)}, u32[]{:S(2)}, u32[]{:S(2)}) async-start(f32[8,32,2048]{2,1,0:T(8,128)} %convolution_bitcast_fusion), calls=%async_computation.1 | async-start | bytes 4194304 | tf_op jit(solution)/shard_map/all_to_all | solution.py:173
  62.2 52.9 %copy-start.573 = (f32[256]{0:T(256)}, f32[256]{0:T(256)S(1)}, u32[]{:S(2)}) copy-start(f32[256]{0:T(256)S(1)} %multiply_multiply_fusion.64) | copy-start | bytes 3076
  62.2 52.8 %copy-start.473 = (f32[32,64]{1,0:T(8,128)}, f32[32,64]{1,0:T(8,128)S(1)}, u32[]{:S(2)}) copy-start(f32[32,64]{1,0:T(8,128)S(1)} %broadcast_add_fusion) | copy-start | bytes 24580
  149.4 52.1 %all-to-all-start.2 = ((f32[32,8,2048]{2,0,1:T(8,128)}), f32[32,8,2048]{2,0,1:T(8,128)S(1)}, u32[]{:S(2)}, u32[]{:S(2)}) async-start(f32[32,8,2048]{2,0,1:T(8,128)} %reshape.2035), calls=%async_computation.2 | async-start | bytes 4194304 | tf_op jit(solution)/shard_map/all_to_all | solution.py:176
  153.6 59.7 %copy-start.503 = (s32[4,64]{1,0:T(4,128)}, s32[4,64]{1,0:T(4,128)S(1)}, u32[]{:S(2)}) copy-start(s32[4,64]{1,0:T(4,128)S(1)} %add_add_fusion.9) | copy-start | bytes 3076
  226.2 29.2 %all-to-all-start.3 = ((f32[4,64,2048]{2,1,0:T(8,128)}), f32[4,64,2048]{2,1,0:T(8,128)S(1)}, u32[]{:S(2)}, u32[]{:S(2)}) async-start(f32[4,64,2048]{2,1,0:T(8,128)} %pad_maximum_fusion), calls=%async_computation.3 | async-start | bytes 4194304 | tf_op jit(solution)/shard_map/all_to_all | solution.py:180
  231.3 134.8 %copy-start.4 = (f32[8,2,8,128]{3,1,2,0:T(2,128)}, f32[8,2,8,128]{3,1,2,0:T(2,128)S(1)}, u32[]{:S(2)}) copy-start(f32[8,2,8,128]{3,1,2,0:T(2,128)S(1)} %copy.941) | copy-start | bytes 196612
  232.2 80.0 %copy-start.413 = (f32[2048]{0:T(1024)}, f32[2048]{0:T(1024)S(1)}, u32[]{:S(2)}) copy-start(f32[2048]{0:T(1024)S(1)} %get-tuple-element.2775) | copy-start | bytes 24580
  232.2 83.9 %copy-start.411 = (f32[2048]{0:T(1024)}, f32[2048]{0:T(1024)S(1)}, u32[]{:S(2)}) copy-start(f32[2048]{0:T(1024)S(1)} %get-tuple-element.2776) | copy-start | bytes 24580
  232.2 79.9 %copy-start.459 = (f32[2048]{0:T(1024)}, f32[2048]{0:T(1024)S(1)}, u32[]{:S(2)}) copy-start(f32[2048]{0:T(1024)S(1)} %get-tuple-element.3235) | copy-start | bytes 24580
  232.3 79.9 %copy-start.461 = (f32[2048]{0:T(1024)}, f32[2048]{0:T(1024)S(1)}, u32[]{:S(2)}) copy-start(f32[2048]{0:T(1024)S(1)} %get-tuple-element.3233) | copy-start | bytes 24580
  232.3 79.9 %copy-start.463 = (f32[2048]{0:T(1024)}, f32[2048]{0:T(1024)S(1)}, u32[]{:S(2)}) copy-start(f32[2048]{0:T(1024)S(1)} %get-tuple-element.3231) | copy-start | bytes 24580
  232.3 79.9 %copy-start.465 = (f32[2048]{0:T(1024)}, f32[2048]{0:T(1024)S(1)}, u32[]{:S(2)}) copy-start(f32[2048]{0:T(1024)S(1)} %get-tuple-element.3229) | copy-start | bytes 24580
  232.3 79.9 %copy-start.467 = (f32[2048]{0:T(1024)}, f32[2048]{0:T(1024)S(1)}, u32[]{:S(2)}) copy-start(f32[2048]{0:T(1024)S(1)} %get-tuple-element.3227) | copy-start | bytes 24580
  232.3 83.7 %copy-start.449 = (f32[2048]{0:T(1024)}, f32[2048]{0:T(1024)S(1)}, u32[]{:S(2)}) copy-start(f32[2048]{0:T(1024)S(1)} %get-tuple-element.3236) | copy-start | bytes 24580
  232.3 83.7 %copy-start.451 = (f32[2048]{0:T(1024)}, f32[2048]{0:T(1024)S(1)}, u32[]{:S(2)}) copy-start(f32[2048]{0:T(1024)S(1)} %get-tuple-element.3234) | copy-start | bytes 24580
  232.3 83.7 %copy-start.453 = (f32[2048]{0:T(1024)}, f32[2048]{0:T(1024)S(1)}, u32[]{:S(2)}) copy-start(f32[2048]{0:T(1024)S(1)} %get-tuple-element.3232) | copy-start | bytes 24580
  232.3 83.7 %copy-start.455 = (f32[2048]{0:T(1024)}, f32[2048]{0:T(1024)S(1)}, u32[]{:S(2)}) copy-start(f32[2048]{0:T(1024)S(1)} %get-tuple-element.3230) | copy-start | bytes 24580
  232.3 83.7 %copy-start.457 = (f32[2048]{0:T(1024)}, f32[2048]{0:T(1024)S(1)}, u32[]{:S(2)}) copy-start(f32[2048]{0:T(1024)S(1)} %get-tuple-element.3228) | copy-start | bytes 24580
  270.0 226.4 %copy-start = (f32[32,64,256]{2,1,0:T(8,128)}, f32[32,64,256]{2,1,0:T(8,128)S(1)}, u32[]{:S(2)}) copy-start(f32[32,64,256]{2,1,0:T(8,128)S(1)} %fusion.1202) | copy-start | bytes 6291460
  272.1 42.1 %copy-start.469 = (f32[2048]{0:T(1024)}, f32[2048]{0:T(1024)S(1)}, u32[]{:S(2)}) copy-start(f32[2048]{0:T(1024)S(1)} %get-tuple-element.3273) | copy-start | bytes 24580
  272.1 42.1 %copy-start.471 = (f32[2048]{0:T(1024)}, f32[2048]{0:T(1024)S(1)}, u32[]{:S(2)}) copy-start(f32[2048]{0:T(1024)S(1)} %get-tuple-element.3275) | copy-start | bytes 24580
  314.2 27.4 %copy-start.17 = (f32[17,2048]{1,0:T(8,128)}, f32[17,2048]{1,0:T(8,128)S(1)}, u32[]{:S(2)}) copy-start(f32[17,2048]{1,0:T(8,128)S(1)} %get-tuple-element.2771) | copy-start | bytes 417796
  314.2 29.6 %copy-start.19 = (f32[17,2048]{1,0:T(8,128)}, f32[17,2048]{1,0:T(8,128)S(1)}, u32[]{:S(2)}) copy-start(f32[17,2048]{1,0:T(8,128)S(1)} %get-tuple-element.2770) | copy-start | bytes 417796
  314.2 31.3 %copy-start.21 = (f32[17,2048]{1,0:T(8,128)}, f32[17,2048]{1,0:T(8,128)S(1)}, u32[]{:S(2)}) copy-start(f32[17,2048]{1,0:T(8,128)S(1)} %get-tuple-element.2769) | copy-start | bytes 417796
  314.2 33.0 %copy-start.23 = (f32[17,2048]{1,0:T(8,128)}, f32[17,2048]{1,0:T(8,128)S(1)}, u32[]{:S(2)}) copy-start(f32[17,2048]{1,0:T(8,128)S(1)} %get-tuple-element.2768) | copy-start | bytes 417796
  314.2 34.7 %copy-start.25 = (f32[17,2048]{1,0:T(8,128)}, f32[17,2048]{1,0:T(8,128)S(1)}, u32[]{:S(2)}) copy-start(f32[17,2048]{1,0:T(8,128)S(1)} %get-tuple-element.2767) | copy-start | bytes 417796
  314.2 36.4 %copy-start.27 = (f32[17,2048]{1,0:T(8,128)}, f32[17,2048]{1,0:T(8,128)S(1)}, u32[]{:S(2)}) copy-start(f32[17,2048]{1,0:T(8,128)S(1)} %get-tuple-element.2766) | copy-start | bytes 417796
  314.2 38.1 %copy-start.29 = (f32[17,2048]{1,0:T(8,128)}, f32[17,2048]{1,0:T(8,128)S(1)}, u32[]{:S(2)}) copy-start(f32[17,2048]{1,0:T(8,128)S(1)} %get-tuple-element.2765) | copy-start | bytes 417796
  314.2 39.8 %copy-start.33 = (f32[17,2048]{1,0:T(8,128)}, f32[17,2048]{1,0:T(8,128)S(1)}, u32[]{:S(2)}) copy-start(f32[17,2048]{1,0:T(8,128)S(1)} %get-tuple-element.2764) | copy-start | bytes 417796
  318.0 26.6 %copy-start.59 = (f32[17,2048]{1,0:T(8,128)}, f32[17,2048]{1,0:T(8,128)S(1)}, u32[]{:S(2)}) copy-start(f32[17,2048]{1,0:T(8,128)S(1)} %get-tuple-element.2800) | copy-start | bytes 417796
  318.0 28.4 %copy-start.61 = (f32[17,2048]{1,0:T(8,128)}, f32[17,2048]{1,0:T(8,128)S(1)}, u32[]{:S(2)}) copy-start(f32[17,2048]{1,0:T(8,128)S(1)} %get-tuple-element.2799) | copy-start | bytes 417796
  318.0 30.1 %copy-start.63 = (f32[17,2048]{1,0:T(8,128)}, f32[17,2048]{1,0:T(8,128)S(1)}, u32[]{:S(2)}) copy-start(f32[17,2048]{1,0:T(8,128)S(1)} %get-tuple-element.2798) | copy-start | bytes 417796
  318.0 31.8 %copy-start.65 = (f32[17,2048]{1,0:T(8,128)}, f32[17,2048]{1,0:T(8,128)S(1)}, u32[]{:S(2)}) copy-start(f32[17,2048]{1,0:T(8,128)S(1)} %get-tuple-element.2797) | copy-start | bytes 417796
  318.0 33.4 %copy-start.67 = (f32[17,2048]{1,0:T(8,128)}, f32[17,2048]{1,0:T(8,128)S(1)}, u32[]{:S(2)}) copy-start(f32[17,2048]{1,0:T(8,128)S(1)} %get-tuple-element.2796) | copy-start | bytes 417796
  318.0 35.2 %copy-start.69 = (f32[17,2048]{1,0:T(8,128)}, f32[17,2048]{1,0:T(8,128)S(1)}, u32[]{:S(2)}) copy-start(f32[17,2048]{1,0:T(8,128)S(1)} %get-tuple-element.2795) | copy-start | bytes 417796
  318.1 36.8 %copy-start.73 = (f32[17,2048]{1,0:T(8,128)}, f32[17,2048]{1,0:T(8,128)S(1)}, u32[]{:S(2)}) copy-start(f32[17,2048]{1,0:T(8,128)S(1)} %get-tuple-element.2794) | copy-start | bytes 417796
  366.1 113.2 %copy-start.6 = (f32[4,2,8,128]{3,1,2,0:T(2,128)S(1)}, f32[4,2,8,128]{3,1,2,0:T(2,128)}, u32[]{:S(2)}) copy-start(f32[4,2,8,128]{3,1,2,0:T(2,128)} %copy.943) | copy-start | bytes 98308
  366.1 113.2 %copy-start.84 = (f32[4,2,8,128]{3,1,2,0:T(2,128)S(1)}, f32[4,2,8,128]{3,1,2,0:T(2,128)}, u32[]{:S(2)}) copy-start(f32[4,2,8,128]{3,1,2,0:T(2,128)} %copy.942) | copy-start | bytes 98308
  366.2 55.0 %copy-start.576 = (f32[17]{0:T(128)}, f32[17]{0:T(128)S(1)}, u32[]{:S(2)}) copy-start(f32[17]{0:T(128)S(1)} %multiply_bitcast_fusion.4) | copy-start | bytes 208 | tf_op jit(solution)/shard_map/cond
  366.2 49.7 %copy-start.570 = (f32[17]{0:T(128)}, f32[17]{0:T(128)S(1)}, u32[]{:S(2)}) copy-start(f32[17]{0:T(128)S(1)} %get-tuple-element.2867) | copy-start | bytes 208 | tf_op jit(solution)/shard_map/cond
  368.0 62.1 %copy-start.477 = (f32[16384]{0:T(1024)}, f32[16384]{0:T(1024)S(1)}, u32[]{:S(2)}) copy-start(f32[16384]{0:T(1024)S(1)} %get-tuple-element.2621) | copy-start | bytes 196612 | tf_op jit(solution)/shard_map/cond
  369.0 40.6 %copy-start.92 = (f32[16384]{0:T(1024)}, f32[16384]{0:T(1024)S(1)}, u32[]{:S(2)}) copy-start(f32[16384]{0:T(1024)S(1)} %get-tuple-element.2828) | copy-start | bytes 196612 | tf_op jit(solution)/shard_map/cond
  369.0 46.9 %copy-start.94 = (f32[16384]{0:T(1024)}, f32[16384]{0:T(1024)S(1)}, u32[]{:S(2)}) copy-start(f32[16384]{0:T(1024)S(1)} %get-tuple-element.2830) | copy-start | bytes 196612 | tf_op jit(solution)/shard_map/cond
  369.0 46.9 %copy-start.96 = (f32[16384]{0:T(1024)}, f32[16384]{0:T(1024)S(1)}, u32[]{:S(2)}) copy-start(f32[16384]{0:T(1024)S(1)} %get-tuple-element.2832) | copy-start | bytes 196612 | tf_op jit(solution)/shard_map/cond
  369.1 64.2 %copy-start.483 = (f32[16384]{0:T(1024)}, f32[16384]{0:T(1024)S(1)}, u32[]{:S(2)}) copy-start(f32[16384]{0:T(1024)S(1)} %get-tuple-element.2862) | copy-start | bytes 196612 | tf_op jit(solution)/shard_map/cond
  551.3 65.0 %copy-start.80 = (f32[17,2048]{1,0:T(8,128)S(1)}, f32[17,2048]{1,0:T(8,128)}, u32[]{:S(2)}) copy-start(f32[17,2048]{1,0:T(8,128)} %copy-done.79) | copy-start | bytes 417796
  551.3 65.2 %copy-start.78 = (f32[17,2048]{1,0:T(8,128)S(1)}, f32[17,2048]{1,0:T(8,128)}, u32[]{:S(2)}) copy-start(f32[17,2048]{1,0:T(8,128)} %copy-done.77) | copy-start | bytes 417796
  551.4 65.5 %copy-start.76 = (f32[17,2048]{1,0:T(8,128)S(1)}, f32[17,2048]{1,0:T(8,128)}, u32[]{:S(2)}) copy-start(f32[17,2048]{1,0:T(8,128)} %copy-done.75) | copy-start | bytes 417796
  551.4 65.7 %copy-start.72 = (f32[17,2048]{1,0:T(8,128)S(1)}, f32[17,2048]{1,0:T(8,128)}, u32[]{:S(2)}) copy-start(f32[17,2048]{1,0:T(8,128)} %copy-done.71) | copy-start | bytes 417796
  551.4 65.9 %copy-start.74 = (f32[17,2048]{1,0:T(8,128)S(1)}, f32[17,2048]{1,0:T(8,128)}, u32[]{:S(2)}) copy-start(f32[17,2048]{1,0:T(8,128)} %copy-done.73) | copy-start | bytes 417796
  551.4 66.2 %copy-start.70 = (f32[17,2048]{1,0:T(8,128)S(1)}, f32[17,2048]{1,0:T(8,128)}, u32[]{:S(2)}) copy-start(f32[17,2048]{1,0:T(8,128)} %copy-done.69) | copy-start | bytes 417796
  551.4 66.4 %copy-start.68 = (f32[17,2048]{1,0:T(8,128)S(1)}, f32[17,2048]{1,0:T(8,128)}, u32[]{:S(2)}) copy-start(f32[17,2048]{1,0:T(8,128)} %copy-done.67) | copy-start | bytes 417796
  551.4 66.6 %copy-start.66 = (f32[17,2048]{1,0:T(8,128)S(1)}, f32[17,2048]{1,0:T(8,128)}, u32[]{:S(2)}) copy-start(f32[17,2048]{1,0:T(8,128)} %copy-done.65) | copy-start | bytes 417796
  559.8 58.5 %copy-start.64 = (f32[17,2048]{1,0:T(8,128)S(1)}, f32[17,2048]{1,0:T(8,128)}, u32[]{:S(2)}) copy-start(f32[17,2048]{1,0:T(8,128)} %copy-done.63) | copy-start | bytes 417796
  658.2 49.7 %copy-start.5 = (f32[8,2,8,128]{3,1,2,0:T(2,128)S(1)}, f32[8,2,8,128]{3,1,2,0:T(2,128)}, u32[]{:S(2)}) copy-start(f32[8,2,8,128]{3,1,2,0:T(2,128)} %copy-done.4) | copy-start | bytes 196612
  724.2 82.0 %copy-start.101 = (s32[256]{0:T(256)S(1)}, s32[256]{0:T(256)}, u32[]{:S(2)}) copy-start(s32[256]{0:T(256)} %copy-done.100) | copy-start | bytes 3076
  808.6 26.3 %copy-start.496 = (s32[8,32]{1,0:T(8,128)S(1)}, s32[8,32]{1,0:T(8,128)}, u32[]{:S(2)}) copy-start(s32[8,32]{1,0:T(8,128)} %copy-done.495) | copy-start | bytes 3076
  810.3 27.5 %copy-start.504 = (s32[4,64]{1,0:T(4,128)S(1)}, s32[4,64]{1,0:T(4,128)}, u32[]{:S(2)}) copy-start(s32[4,64]{1,0:T(4,128)} %copy-done.503) | copy-start | bytes 3076
  840.5 15.2 %all-to-all-start.5 = ((f32[8,32,320]{2,1,0:T(8,128)}), f32[8,32,320]{2,1,0:T(8,128)S(1)}, u32[]{:S(2)}, u32[]{:S(2)}) async-start(f32[8,32,320]{2,1,0:T(8,128)} %pad_maximum_fusion.2), calls=%async_computation.5 | async-start | bytes 786432 | tf_op jit(solution)/shard_map/all_to_all | solution.py:173
  (410 other events, 2290.1 us)
